TPU v7x, 32 devices: a whole 2x2x4 slice. The times are simulated.
32 devices in a mesh: seq: 2 (over x), head: 4 (over z), dp: 4 (over y, core).
Axes of the slice: x: 2, y: 2, z: 4, core: 2. Of those that a mesh axis runs over, the one named last changes fastest.
Arguments:
- queries: bfloat16 [4, 512, 64, 128], P('dp', 'seq', 'head'), may hold values from -6 to 6
- keys: bfloat16 [4, 512, 8, 128], P('dp', 'seq', 'head'), may hold values from -6 to 6
- values: bfloat16 [4, 512, 8, 128], P('dp', 'seq', 'head'), may hold values from -6 to 6
- attn_out: bfloat16 [4, 512, 64, 128], P('dp', 'seq', 'head'), may hold values from -6 to 6
- out_grad: bfloat16 [4, 512, 64, 128], P('dp', 'seq', 'head'), may hold values from -6 to 6
- gate_values: float32 [4, 64, 512], P('dp', 'head', 'seq'), may hold values from 0.05 to 0.95
- log_totals: float32 [4, 64, 512], P('dp', 'head', 'seq'), may hold values from 3 to 5
- hidden: bfloat16 [4, 512, 5120], P('dp', 'seq', 'head'), may hold values from -6 to 6
- block_ids: int32 [4, 8, 8, 16], P('dp', 'seq', 'head'), may hold values from 0 to 7, as said below
- block_valid: int32 [4, 8, 8, 16], P('dp', 'seq', 'head'), may hold values from 0 to 1
Outputs:
- query_grad: bfloat16 [4, 512, 64, 128], P('dp', 'seq', 'head')
- key_grad: bfloat16 [4, 512, 8, 128], P('dp', 'seq', 'head')
- value_grad: bfloat16 [4, 512, 8, 128], P('dp', 'seq', 'head')
- gate_weight_grad: float32 [64, 5120], P(None, 'head')
Inputs may be any that keep to these rules, and one draw needn't show every extreme that they name: `block_ids`: for query tile t and key head k, the slots whose block_valid is 1 name distinct blocks of index at most t, among them block t itself and block 0; exactly min(16, t + 1) slots are valid. The ids of the other slots are any blocks, and may repeat a valid one.
All inputs are finite; a program needn't handle non-finite values.
Results may differ from a plain program's by a relative error of at most 0.025.
Values may be sent and summed in bfloat16 or wider, within the bound.
A program may use at most 128 MiB of HBM per device.

v0:
```python
import math

import jax
import jax.numpy as jnp
from jax import lax
from jax.sharding import PartitionSpec as P


def on_device(
    queries,
    keys,
    values,
    attn_out,
    out_grad,
    gate_values,
    log_totals,
    hidden,
    block_ids,
    block_valid,
):
    tokens_here = queries.shape[1]
    heads_here = queries.shape[2]
    kv_heads = keys.shape[2]
    head_width = queries.shape[3]
    group_size = heads_here // kv_heads
    tiles_here = block_ids.shape[1]
    block_rows = tokens_here // tiles_here
    seq_count = lax.axis_size("seq")
    all_blocks = tiles_here * seq_count
    factor = head_width ** (-0.5)
    chosen = block_ids[0]
    usable = block_valid[0] > 0
    head_rows = jnp.arange(kv_heads, dtype=jnp.int32)[None, :, None]
    offsets = jnp.arange(block_rows, dtype=jnp.int32)
    whole_keys, whole_values = (
        lax.all_gather(keys, "seq", axis=1, tiled=True),
        lax.all_gather(values, "seq", axis=1, tiled=True),
    )
    key_sel = whole_keys[0].reshape(all_blocks, block_rows, kv_heads, head_width)[
        chosen, :, head_rows, :
    ]
    value_sel = whole_values[0].reshape(all_blocks, block_rows, kv_heads, head_width)[
        chosen, :, head_rows, :
    ]
    query_tiles = queries[0].reshape(tiles_here, block_rows, kv_heads, group_size, head_width)
    output_tiles = attn_out[0].reshape(tiles_here, block_rows, kv_heads, group_size, head_width)
    upstream_tiles = out_grad[0].reshape(tiles_here, block_rows, kv_heads, group_size, head_width)
    gate_tiles = jnp.transpose(
        gate_values[0].reshape(kv_heads, group_size, tiles_here, block_rows), (2, 0, 1, 3)
    )
    total_tiles = jnp.transpose(
        log_totals[0].reshape(kv_heads, group_size, tiles_here, block_rows), (2, 0, 1, 3)
    )
    tile_numbers = lax.axis_index("seq") * tiles_here + jnp.arange(tiles_here, dtype=jnp.int32)

    def tile_math(tile_items):
        (
            tile_number,
            query_tile,
            output_tile,
            upstream,
            gate_tile,
            totals,
            picked,
            usable_tile,
            key_tile,
            value_tile,
        ) = tile_items
        gates_by_row = jnp.transpose(gate_tile, (2, 0, 1))
        grad_output = (gates_by_row[..., None] * upstream.astype(jnp.float32)).astype(jnp.bfloat16)
        output_wide = output_tile.astype(jnp.float32)
        row_delta = jnp.transpose(
            jnp.sum(grad_output.astype(jnp.float32) * output_wide, axis=-1), (1, 2, 0)
        )
        gate_grad = jnp.sum(upstream.astype(jnp.float32) * output_wide, axis=-1)
        logit_grad = (gate_grad * gates_by_row * (1.0 - gates_by_row)).astype(jnp.bfloat16)
        scores = (
            jnp.einsum("ikgd,knjd->kginj", query_tile, key_tile, preferred_element_type=jnp.float32)
            * factor
        )
        query_pos = tile_number * block_rows + offsets
        key_pos = picked[..., None] * block_rows + offsets
        allowed = usable_tile[:, None, :, None] & (
            key_pos[:, None, :, :] <= query_pos[None, :, None, None]
        )
        probability = jnp.where(allowed[:, None], jnp.exp(scores - totals[..., None, None]), 0.0)
        prob_grad = jnp.einsum(
            "ikgd,knjd->kginj", grad_output, value_tile, preferred_element_type=jnp.float32
        )
        dscore = (probability * (prob_grad - row_delta[..., None, None])).astype(jnp.bfloat16)
        prob_low = probability.astype(jnp.bfloat16)
        query_part = (
            jnp.einsum("kginj,knjd->ikgd", dscore, key_tile, preferred_element_type=jnp.float32)
            * factor
        ).astype(jnp.bfloat16)
        key_part = (
            jnp.einsum("kginj,ikgd->knjd", dscore, query_tile, preferred_element_type=jnp.float32)
            * factor
        )
        value_part = jnp.einsum(
            "kginj,ikgd->knjd", prob_low, grad_output, preferred_element_type=jnp.float32
        )
        return (query_part, logit_grad, jnp.concatenate([key_part, value_part], axis=-1))

    def tile_step(partial_value, tile_items):
        query_part, logit_grad, paired = tile_math(tile_items)
        return (partial_value, (query_part, logit_grad, paired))

    tile_items = (
        tile_numbers,
        query_tiles,
        output_tiles,
        upstream_tiles,
        gate_tiles,
        total_tiles,
        chosen,
        usable,
        key_sel,
        value_sel,
    )
    unused, (query_parts, logit_parts, paired_all) = lax.scan(
        tile_step, jnp.zeros((), jnp.float32), tile_items
    )
    span_blocks = tokens_here * lax.axis_size("seq") // block_rows
    target = chosen
    target = jnp.where((target >= 0) & (target < span_blocks), target, span_blocks)
    holder = jnp.zeros((span_blocks, block_rows, kv_heads, 2 * head_width), jnp.float32)
    holder = holder.at[target, :, head_rows, :].add(paired_all, mode="drop")
    summed = lax.psum_scatter(
        holder.reshape(tokens_here * lax.axis_size("seq"), kv_heads, 2 * head_width).astype(
            jnp.bfloat16
        ),
        "seq",
        scatter_dimension=0,
        tiled=True,
    ).astype(jnp.float32)
    query_grad = query_parts.reshape(1, tokens_here, heads_here, head_width)
    logit_rows = jnp.transpose(logit_parts.reshape(tokens_here, heads_here))[None]
    every_logit = lax.all_gather(logit_rows, "head", axis=1, tiled=True)
    weight_part = jnp.dot(every_logit[0], hidden[0], preferred_element_type=jnp.float32)
    weight_scale = 1.0 / math.sqrt(lax.axis_size("dp") * seq_count * tokens_here)
    gate_weight_grad = lax.psum(weight_part, ("seq", "dp")) * weight_scale
    key_grad = summed[None, :, :, :head_width].astype(jnp.bfloat16)
    value_grad = summed[None, :, :, head_width:].astype(jnp.bfloat16)
    return (query_grad, key_grad, value_grad, gate_weight_grad)


def solution(mesh):
    return jax.shard_map(
        on_device,
        mesh=mesh,
        in_specs=(
            P("dp", "seq", "head", None),
            P("dp", "seq", "head", None),
            P("dp", "seq", "head", None),
            P("dp", "seq", "head", None),
            P("dp", "seq", "head", None),
            P("dp", "head", "seq"),
            P("dp", "head", "seq"),
            P("dp", "seq", "head"),
            P("dp", "seq", "head", None),
            P("dp", "seq", "head", None),
        ),
        out_specs=(
            P("dp", "seq", "head", None),
            P("dp", "seq", "head", None),
            P("dp", "seq", "head", None),
            P(None, "head"),
        ),
        check_vma=False,
    )
```

profile of v0, /device:TPU:0, one launch (start us, length us, event | category | flops | bytes accessed | tf_op | source)
XLA Modules:
  0.0 180.2 jit_solution(4722716227157090044)
XLA Ops:
  8.1 0.9 copy.32
  9.0 7.1 %all_gather.9 = bf16[1,512,2,128]{3,1,2,0:T(8,128)(2,1)S(1)} all-gather(bf16[1,256,2,128]{3,1,2,0:T(8,128)(2,1)S(1)} %copy.32), channel_id=1, replica_groups=mesh['seq'=2,'head'=4,'dp'=4] {'seq'}, dimensions={1}, use_global_device_ids=true | all-gather | bytes 393216 | tf_op jit(solution)/shard_map/all_gather | solution.py:36
  18.5 0.9 copy.35
  19.4 5.6 %all_gather.10 = bf16[1,512,2,128]{3,1,2,0:T(8,128)(2,1)S(1)} all-gather(bf16[1,256,2,128]{3,1,2,0:T(8,128)(2,1)S(1)} %copy.35), channel_id=1, replica_groups=mesh['seq'=2,'head'=4,'dp'=4] {'seq'}, dimensions={1}, use_global_device_ids=true | all-gather | bytes 393216 | tf_op jit(solution)/shard_map/all_gather | solution.py:37
  25.1 1.1 gather_fusion
  26.1 2.3 %gather_fusion.1 = bf16[128,64,128]{2,1,0:T(8,128)(2,1)} fusion(bf16[8,64,2,128]{3,1,2,0:T(8,128)(2,1)S(1)} %copy.36, s32[128]{0:T(128)S(1)} %reshape.124), kind=kCustom, calls=%fused_computation.1 | custom fusion | bytes 4195328 | tf_op jit(solution)/shard_map/gather | solution.py:42
  28.6 69.9 %while.16 = (s32[]{:T(128)}, bf16[4,64,2,8,128]{4,3,2,1,0:T(8,128)(2,1)}, bf16[4,64,2,8]{1,3,2,0:T(8,128)(2,1)S(1)}, f32[4,2,16,64,256]{4,3,2,1,0:T(8,128)}, bf1...) while((s32[]{:T(128)}, ...), condition=%wide.region_3.4_spmd.clone.clone, body=%wide.region_0.3_spmd.clone.clone.sunk | while | flops 1355944064 | bytes 33248452 | solution.py:121
  28.6 1.0 constant_dynamic-slice_fusion.10
  29.6 1.3 fusion.78
  30.8 1.1 constant_dynamic-slice_fusion.11
  35.0 4.0 %fusion.82 = bf16[2,8,64,16,64]{2,4,1,3,0:T(8,128)(2,1)S(1)} fusion(f32[2,16,64,64,8]{3,2,4,1,0:T(8,128)S(1)} %fusion.78, f32[2,8,64]{2,1,0:T(8,128)S(1)} %bitcast.222, f32[2,8,64]{2,1,0:T(8,128)S(1)} %bitcast.223, pred[2,64,16,64]{1,3,2,0:T(8,128)(4,1)S(1)} %compare_and_fusion.2, bf16[4,2,16,64,128]{4,3,2,1,0:T(8,128)(2,1)} %get-tuple-element.380, ...), kind=kOutput, calls=%fused_computation.6.clone.1 | convolution fusion | flops 275120128 | bytes 7221252 | tf_op jit(solution)/shard_map/while/body/eval_jaxpr/ikgd,knjd->kginj/dot_general | solution.py:87
  39.0 1.3 fusion.83
  40.3 0.9 copy_dynamic-update-slice_fusion.2
  41.2 2.4 %fusion.85 = f32[2,16,64,128]{3,2,1,0:T(8,128)S(1)} fusion(f32[2,16,64,64,8]{3,2,4,1,0:T(8,128)S(1)} %fusion.78, f32[2,8,64]{2,1,0:T(8,128)S(1)} %bitcast.224, pred[2,64,16,64]{1,3,2,0:T(8,128)(4,1)S(1)} %compare_and_fusion.2, f32[64,2,8]{0,2,1:T(8,128)S(1)} %bitcast.216, bf16[1,64,2,8,128]{4,3,2,1,0:T(8,128)(2,1)S(1)} %get-tuple-element.332), kind=kOutput, calls=%fused_computation.17.clone.1 | convolution fusion | flops 273022976 | bytes 5644288 | tf_op jit(solution)/shard_map/while/body/eval_jaxpr/kginj,ikgd->knjd/dot_general | solution.py:100
  43.6 0.9 fusion.86
  44.6 1.5 fusion.87
  46.1 1.0 constant_dynamic-slice_fusion.10
  47.0 1.3 fusion.78
  48.3 1.1 constant_dynamic-slice_fusion.11
  52.4 4.0 %fusion.82 = bf16[2,8,64,16,64]{2,4,1,3,0:T(8,128)(2,1)S(1)} fusion(f32[2,16,64,64,8]{3,2,4,1,0:T(8,128)S(1)} %fusion.78, f32[2,8,64]{2,1,0:T(8,128)S(1)} %bitcast.222, f32[2,8,64]{2,1,0:T(8,128)S(1)} %bitcast.223, pred[2,64,16,64]{1,3,2,0:T(8,128)(4,1)S(1)} %compare_and_fusion.2, bf16[4,2,16,64,128]{4,3,2,1,0:T(8,128)(2,1)} %get-tuple-element.380, ...), kind=kOutput, calls=%fused_computation.6.clone.1 | convolution fusion | flops 275120128 | bytes 7221252 | tf_op jit(solution)/shard_map/while/body/eval_jaxpr/ikgd,knjd->kginj/dot_general | solution.py:87
  56.5 1.3 fusion.83
  57.8 0.9 copy_dynamic-update-slice_fusion.2
  58.7 2.4 %fusion.85 = f32[2,16,64,128]{3,2,1,0:T(8,128)S(1)} fusion(f32[2,16,64,64,8]{3,2,4,1,0:T(8,128)S(1)} %fusion.78, f32[2,8,64]{2,1,0:T(8,128)S(1)} %bitcast.224, pred[2,64,16,64]{1,3,2,0:T(8,128)(4,1)S(1)} %compare_and_fusion.2, f32[64,2,8]{0,2,1:T(8,128)S(1)} %bitcast.216, bf16[1,64,2,8,128]{4,3,2,1,0:T(8,128)(2,1)S(1)} %get-tuple-element.332), kind=kOutput, calls=%fused_computation.17.clone.1 | convolution fusion | flops 273022976 | bytes 5644288 | tf_op jit(solution)/shard_map/while/body/eval_jaxpr/kginj,ikgd->knjd/dot_general | solution.py:100
  61.1 0.9 fusion.86
  62.1 1.4 fusion.87
  63.5 1.0 constant_dynamic-slice_fusion.10
  64.5 1.3 fusion.78
  65.7 1.1 constant_dynamic-slice_fusion.11
  69.9 4.0 %fusion.82 = bf16[2,8,64,16,64]{2,4,1,3,0:T(8,128)(2,1)S(1)} fusion(f32[2,16,64,64,8]{3,2,4,1,0:T(8,128)S(1)} %fusion.78, f32[2,8,64]{2,1,0:T(8,128)S(1)} %bitcast.222, f32[2,8,64]{2,1,0:T(8,128)S(1)} %bitcast.223, pred[2,64,16,64]{1,3,2,0:T(8,128)(4,1)S(1)} %compare_and_fusion.2, bf16[4,2,16,64,128]{4,3,2,1,0:T(8,128)(2,1)} %get-tuple-element.380, ...), kind=kOutput, calls=%fused_computation.6.clone.1 | convolution fusion | flops 275120128 | bytes 7221252 | tf_op jit(solution)/shard_map/while/body/eval_jaxpr/ikgd,knjd->kginj/dot_general | solution.py:87
  73.9 1.3 fusion.83
  75.2 0.9 copy_dynamic-update-slice_fusion.2
  76.1 2.4 %fusion.85 = f32[2,16,64,128]{3,2,1,0:T(8,128)S(1)} fusion(f32[2,16,64,64,8]{3,2,4,1,0:T(8,128)S(1)} %fusion.78, f32[2,8,64]{2,1,0:T(8,128)S(1)} %bitcast.224, pred[2,64,16,64]{1,3,2,0:T(8,128)(4,1)S(1)} %compare_and_fusion.2, f32[64,2,8]{0,2,1:T(8,128)S(1)} %bitcast.216, bf16[1,64,2,8,128]{4,3,2,1,0:T(8,128)(2,1)S(1)} %get-tuple-element.332), kind=kOutput, calls=%fused_computation.17.clone.1 | convolution fusion | flops 273022976 | bytes 5644288 | tf_op jit(solution)/shard_map/while/body/eval_jaxpr/kginj,ikgd->knjd/dot_general | solution.py:100
  78.5 0.9 fusion.86
  79.5 1.5 fusion.87
  81.0 1.0 constant_dynamic-slice_fusion.10
  81.9 1.3 fusion.78
  83.2 1.1 constant_dynamic-slice_fusion.11
  87.3 4.0 %fusion.82 = bf16[2,8,64,16,64]{2,4,1,3,0:T(8,128)(2,1)S(1)} fusion(f32[2,16,64,64,8]{3,2,4,1,0:T(8,128)S(1)} %fusion.78, f32[2,8,64]{2,1,0:T(8,128)S(1)} %bitcast.222, f32[2,8,64]{2,1,0:T(8,128)S(1)} %bitcast.223, pred[2,64,16,64]{1,3,2,0:T(8,128)(4,1)S(1)} %compare_and_fusion.2, bf16[4,2,16,64,128]{4,3,2,1,0:T(8,128)(2,1)} %get-tuple-element.380, ...), kind=kOutput, calls=%fused_computation.6.clone.1 | convolution fusion | flops 275120128 | bytes 7221252 | tf_op jit(solution)/shard_map/while/body/eval_jaxpr/ikgd,knjd->kginj/dot_general | solution.py:87
  91.4 1.3 fusion.83
  93.6 2.4 %fusion.85 = f32[2,16,64,128]{3,2,1,0:T(8,128)S(1)} fusion(f32[2,16,64,64,8]{3,2,4,1,0:T(8,128)S(1)} %fusion.78, f32[2,8,64]{2,1,0:T(8,128)S(1)} %bitcast.224, pred[2,64,16,64]{1,3,2,0:T(8,128)(4,1)S(1)} %compare_and_fusion.2, f32[64,2,8]{0,2,1:T(8,128)S(1)} %bitcast.216, bf16[1,64,2,8,128]{4,3,2,1,0:T(8,128)(2,1)S(1)} %get-tuple-element.332), kind=kOutput, calls=%fused_computation.17.clone.1 | convolution fusion | flops 273022976 | bytes 5644288 | tf_op jit(solution)/shard_map/while/body/eval_jaxpr/kginj,ikgd->knjd/dot_general | solution.py:100
  96.0 0.9 fusion.86
  96.9 1.5 fusion.87
  98.5 13.6 %all-gather = bf16[64,256]{1,0:T(8,128)(2,1)S(1)} all-gather(bf16[16,256]{1,0:T(8,128)(2,1)S(1)} %bitcast.227), channel_id=2, replica_groups=mesh['seq'=2,'head'=4,'dp'=4] {'head'}, dimensions={0}, use_global_device_ids=true | all-gather | bytes 40960 | tf_op jit(solution)/shard_map/all_gather | solution.py:139
  112.2 1.0 fusion.42
  113.4 19.1 %scatter_fusion = f32[8,64,2,256]{3,1,2,0:T(8,128)S(1)} fusion(f32[8,64,2,256]{3,1,2,0:T(8,128)S(1)} %broadcast_in_dim.53, s32[128]{0:T(128)S(1)} %reshape.136, f32[128,64,256]{2,1,0:T(8,128)} %bitcast.210), kind=kCustom, calls=%fused_computation.2 | custom fusion | flops 2097152 | bytes 25166848 | tf_op jit(solution)/shard_map/scatter-add | solution.py:128
  133.4 35.1 %all-reduce.2.cloned.1.call-done = f32[64,1280]{1,0:T(8,128)} async-done(((f32[64,1280]{1,0:T(8,128)}), f32[64,1280]{1,0:T(8,128)}) %all-reduce.2.cloned.1.call-update) | async-done | bytes 327696 | tf_op jit(solution)/shard_map/psum | solution.py:142
  168.5 1.7 broadcast_multiply_fusion
  170.2 1.0 slice_bitcast_fusion
  (65 shorter events, 15.7 us)
Async XLA Ops:
  8.0 104.2 %copy-start = (bf16[1,256,1280]{2,1,0:T(8,128)(2,1)S(1)}, bf16[1,256,1280]{2,1,0:T(8,128)(2,1)}, u32[]{:S(2)}) copy-start(bf16[1,256,1280]{2,1,0:T(8,128)(2,1)} %param.19) | copy-start | bytes 1966084
  8.0 20.5 %copy-start.1 = (f32[1,16,256]{2,1,0:T(8,128)S(1)}, f32[1,16,256]{2,1,0:T(8,128)}, u32[]{:S(2)}) copy-start(f32[1,16,256]{2,1,0:T(8,128)} %param.17) | copy-start | bytes 49156
  8.0 160.4 %all-reduce.2.cloned.1.call-start = ((), (), s32[]{:S(2)}) async-start(), calls=%async_computation.2 | async-start | bytes 655360 | tf_op jit(solution)/shard_map/psum | solution.py:142
  113.2 57.0 %reduce-scatter.2.cloned.1.call-start = ((), (), s32[]{:S(2)}) async-start(), calls=%async_computation.1 | async-start | bytes 786432 | tf_op jit(solution)/shard_map/reduce_scatter | solution.py:129
Sparse Core Ops, SparseCore 0:
  113.3 55.1 all-reduce.1
Sparse Core Ops, SparseCore 1:
  133.5 15.6 reduce-scatter.1
where the time goes:
time: 181 us; the launch traced here: 180 us
  matrix products  40.9 us (23%)
  other arithmetic  35.2 us (19%)
  waiting for transfers between devices  35.1 us (19%)
  blocking collectives  26.4 us (15%)
  local copies, waits for them, and re-layouts  24.1 us (13%)
  between operations  15.6 us (9%)
  loops' own time  2.88 us (2%)
    psum x1, waiting for transfers between devices, on_device(): gate_weight_grad = lax.psum(weight_part, ('seq', 'dp')) * weight_scale  35.1 us
    scatter-add x1, other arithmetic, on_device(): holder = holder.at[target, :, head_rows, :].add(paired_all, mode='drop')  19.1 us
    dot_general x4, matrix products, tile_math(): jnp.einsum('ikgd,knjd->kginj', grad_output, value_tile, preferred_element...  16.1 us
    all_gather x1, blocking collectives, on_device(): every_logit = lax.all_gather(logit_rows, 'head', axis=1, tiled=True)  13.6 us
    dynamic_slice x16, local copies, waits for them, and re-layouts, on_device(): lax.scan(tile_step, jnp.zeros((), jnp.float32), tile_items)  10.6 us
    dot_general x4, matrix products, tile_math(): jnp.einsum('kginj,ikgd->knjd', prob_low, grad_output, preferred_element_t...  9.55 us
    all_gather x1, blocking collectives, on_device(): lax.all_gather(keys, 'seq', axis=1, tiled=True)  7.12 us
    dynamic_update_slice x8, other arithmetic, on_device(): lax.scan(tile_step, jnp.zeros((), jnp.float32), tile_items)  5.93 us
  transfers between devices with their start and end apart: 2, of which 1 were waited for; matrix products, arithmetic and copies ran while one was open for 12% of the time, Pallas kernels for 0%

commit v1 on v0

v1 whole, which is shorter than its diff:
```python
import functools
import math

import jax
import jax.numpy as jnp
from jax import lax
from jax.experimental import pallas as pl
from jax.experimental.pallas import tpu as pltpu
from jax.sharding import PartitionSpec as P

F32 = jnp.float32
BF16 = jnp.bfloat16
MASKED = -1e9
NT = (((1,), (1,)), ((), ()))
NN = (((1,), (0,)), ((), ()))
TN = (((0,), (0,)), ((), ()))


def mm(a, b, dims):
    return lax.dot_general(a, b, dims, preferred_element_type=F32)


def split3(x):
    hi = x.astype(BF16).astype(F32)
    mid = (x - hi).astype(BF16).astype(F32)
    lo = (x - hi - mid).astype(BF16).astype(F32)
    return hi, mid, lo


def kernel(
    dims,
    ids_ref, valid_ref, q_ref, ao_ref, og_ref, gate_ref, tot_ref, hid_ref, kv_ref,
    qg_ref, dkv_ref, wg_ref,
    cols, lgt, qaug, doaug, dq_acc, kv_in, kv_acc, g_send, g_recv,
    lg_all, w_own, w_send, w_recv, x_all, o_all,
    kv_ss, kv_rs, g_ss, g_rs, lg_ss, lg_rs, w_ss, w_rs, x_ss, x_rs, o_ss, o_rs,
):
    n_seq, n_head, n_dp, tiles, blk, kvh, group, dh, nsel = dims
    heads = kvh * group
    rows = blk * group
    toks = tiles * blk
    s = lax.axis_index("seq")
    h = lax.axis_index("head")
    d = lax.axis_index("dp")
    root = math.sqrt(dh)
    cexp = math.log2(math.e) / root

    barrier = pltpu.get_barrier_semaphore()
    for name, me, n in (("seq", s, n_seq), ("head", h, n_head), ("dp", d, n_dp)):
        for off in range(1, n):
            pl.semaphore_signal(
                barrier, inc=1, device_id={name: lax.rem(me + off, n)},
                device_id_type=pl.DeviceIdType.MESH)
    pl.semaphore_wait(barrier, n_seq + n_head + n_dp - 3)

    def kv_copy(k, src_s, dst_s):
        return pltpu.make_async_remote_copy(
            src_ref=kv_ref.at[k], dst_ref=kv_in.at[src_s, k],
            send_sem=kv_ss.at[dst_s, k], recv_sem=kv_rs.at[src_s, k],
            device_id={"seq": dst_s}, device_id_type=pl.DeviceIdType.MESH)

    def g_copy(k, src_s, dst_s):
        return pltpu.make_async_remote_copy(
            src_ref=g_send.at[dst_s, k], dst_ref=g_recv.at[src_s, k],
            send_sem=g_ss.at[dst_s, k], recv_sem=g_rs.at[src_s, k],
            device_id={"seq": dst_s}, device_id_type=pl.DeviceIdType.MESH)

    def slot_copy(src, dst, ss, rs, axis, src_i, dst_i):
        return pltpu.make_async_remote_copy(
            src_ref=src, dst_ref=dst.at[src_i],
            send_sem=ss.at[dst_i], recv_sem=rs.at[src_i],
            device_id={axis: dst_i}, device_id_type=pl.DeviceIdType.MESH)

    def loop(lo, hi, fn):
        def step(i, c):
            fn(i)
            return c
        lax.fori_loop(lo, hi, step, 0)

    for k in range(kvh):
        loop(s + 1, n_seq, lambda j: kv_copy(k, s, j).start())

    hi, mid, lo = split3(tot_ref[...] * (-root))
    stack = jnp.concatenate(
        [gate_ref[...], hi, mid, lo, jnp.zeros((128 - 4 * heads, toks), F32)], axis=0)
    cols[...] = jnp.transpose(stack)

    lane = lax.broadcasted_iota(jnp.int32, (rows, 128), 1)
    g_of = lax.rem(lax.broadcasted_iota(jnp.int32, (rows, 128), 0), group)
    pick = (
        lax.broadcasted_iota(jnp.int32, (blk, rows), 0)
        == lax.broadcasted_iota(jnp.int32, (blk, rows), 1) // group
    ).astype(BF16)
    lane1 = lax.broadcasted_iota(jnp.int32, (1, 128), 1)

    def prep(t):
        at = pl.ds(pl.multiple_of(t * blk, blk), blk)
        og = og_ref[at].astype(F32)
        ao = ao_ref[at].astype(F32)
        q = q_ref[at].astype(F32)
        wide = jnp.broadcast_to(cols[at][:, None, :], (blk, group, 128)).reshape(rows, 128)
        x = jnp.zeros((rows, 128), F32)
        for k in range(kvh):
            part = slice(k * group, (k + 1) * group)
            ogk = og[:, part, :].reshape(rows, dh)
            aok = ao[:, part, :].reshape(rows, dh)
            qk = q[:, part, :].reshape(rows, dh)
            mine = lax.rem(lane, heads) == g_of + k * group
            sel = jnp.full((1, 128), MASKED, F32)
            for n in range(nsel):
                b = jnp.where(valid_ref[t, k, n] > 0, ids_ref[t, k, n], -1000)
                sel = jnp.where(lane1 == b + 4 * heads, 0.0, sel)
            gate = jnp.sum(jnp.where(mine & (lane < heads), wide, 0.0), axis=1, keepdims=True)
            tail = jnp.where(
                lane >= 4 * heads, sel, jnp.where(mine & (lane >= heads), wide, 0.0))
            qaug[t, k, :, :dh] = qk.astype(BF16)
            qaug[t, k, :, dh:] = tail.astype(BF16)
            go = (gate * ogk).astype(BF16)
            dl_hi, dl_mid, dl_lo = split3(
                -jnp.sum(go.astype(F32) * aok, axis=1, keepdims=True))
            doaug[t, k, :, :dh] = go
            doaug[t, k, :, dh:] = jnp.where(
                lane == heads, dl_hi,
                jnp.where(lane == heads + 1, dl_mid,
                          jnp.where(lane == heads + 2, dl_lo, 0.0))).astype(BF16)
            lg = jnp.sum(ogk * aok, axis=1, keepdims=True) * gate * (1.0 - gate)
            x = x + jnp.where(lane == g_of + k * group, lg, 0.0)
        lgt[at, :] = mm(pick, x.astype(BF16), NN)

    loop(0, tiles, prep)
    lg_all[h] = jnp.transpose(lgt[...])[:heads].astype(BF16)
    for off in range(1, n_head):
        slot_copy(lg_all.at[h], lg_all, lg_ss, lg_rs, "head", h, lax.rem(h + off, n_head)).start()

    def key_tail(r):
        ln = lax.broadcasted_iota(jnp.int32, (toks, 128), 1)
        bk = lax.broadcasted_iota(jnp.int32, (toks, 128), 0) // blk + r * tiles
        hot = (ln == bk + 4 * heads) | ((ln >= heads) & (ln < 4 * heads))
        return jnp.where(hot, 1.0, 0.0).astype(BF16)

    def pair(kk, vv, tail, t, k, causal):
        nk = kk.shape[0]
        qa = qaug[t, k]
        da = doaug[t, k]
        sc = mm(jnp.concatenate([kk, tail], axis=1), qa, NT)
        p = jnp.exp2(sc * cexp)
        if causal:
            row = lax.broadcasted_iota(jnp.int32, (nk, rows), 0) - (nk - blk)
            tok = lax.broadcasted_iota(jnp.int32, (nk, rows), 1) // group
            p = jnp.where(row <= tok, p, 0.0)
        dp = mm(jnp.concatenate([vv, tail], axis=1), da, NT)
        ds = (p * dp).astype(BF16)
        dq = mm(ds, kk, TN)
        dk = mm(ds, qa[:, :dh], NN)
        dv = mm(p.astype(BF16), da[:, :dh], NN)
        return dq, dk, dv

    own_tail = key_tail(s)

    def local(k):
        for t in range(tiles - 1, -1, -1):
            nk = (t + 1) * blk
            dq, dk, dv = pair(kv_ref[k, 0, :nk], kv_ref[k, 1, :nk], own_tail[:nk], t, k, True)
            dq_acc[t, k] = dq
            if t == tiles - 1:
                kv_acc[k, 0] = dk
                kv_acc[k, 1] = dv
            else:
                kv_acc[k, 0, :nk] += dk
                kv_acc[k, 1, :nk] += dv

    def remote(k):
        def one(i):
            r = s - 1 - i
            kv_copy(k, r, s).wait_recv()
            tail = key_tail(r)
            kk = kv_in[r, k, 0]
            vv = kv_in[r, k, 1]
            dks = dvs = None
            for t in range(tiles):
                dq, dk, dv = pair(kk, vv, tail, t, k, False)
                dq_acc[t, k] += dq
                dks = dk if dks is None else dks + dk
                dvs = dv if dvs is None else dvs + dv
            g_send[r, k, 0] = (dks * (1.0 / root)).astype(BF16)
            g_send[r, k, 1] = dvs.astype(BF16)
            g_copy(k, s, r).start()
        loop(0, s, one)

    for k in range(kvh):
        local(k)

    for off in range(1, n_head):
        j = lax.rem(h + off, n_head)
        slot_copy(lg_all.at[j], lg_all, lg_ss, lg_rs, "head", j, h).wait_recv()
    hq = n_head * heads
    w = mm(lg_all[...].reshape(hq, toks), hid_ref[...], NN)
    part = hq // n_dp
    for j in range(n_dp):
        w_own[j] = w[j * part:(j + 1) * part]
        w_send[j] = w[j * part:(j + 1) * part].astype(BF16)
    for off in range(1, n_dp):
        j = lax.rem(d + off, n_dp)
        slot_copy(w_send.at[j], w_recv, w_ss, w_rs, "dp", d, j).start()

    remote(0)

    total = w_own[d]
    for off in range(1, n_dp):
        j = lax.rem(d + off, n_dp)
        slot_copy(w_send.at[d], w_recv, w_ss, w_rs, "dp", j, d).wait_recv()
        total = total + w_recv[j].astype(F32)
    x_all[s] = total.astype(BF16)
    for off in range(1, n_seq):
        slot_copy(x_all.at[s], x_all, x_ss, x_rs, "seq", s, lax.rem(s + off, n_seq)).start()

    for k in range(1, kvh):
        remote(k)

    for off in range(1, n_seq):
        j = lax.rem(s + off, n_seq)
        slot_copy(x_all.at[j], x_all, x_ss, x_rs, "seq", j, s).wait_recv()
    total = x_all[0].astype(F32)
    for j in range(1, n_seq):
        total = total + x_all[j].astype(F32)
    o_all[d] = (total * (1.0 / math.sqrt(n_dp * n_seq * toks))).astype(BF16)
    for off in range(1, n_dp):
        slot_copy(o_all.at[d], o_all, o_ss, o_rs, "dp", d, lax.rem(d + off, n_dp)).start()

    for t in range(tiles):
        qg_ref[t * blk:(t + 1) * blk] = jnp.concatenate(
            [dq_acc[t, k].reshape(blk, group, dh) for k in range(kvh)], axis=1
        ).__mul__(1.0 / root).astype(BF16)

    for k in range(kvh):
        kv_acc[k, 0] = (kv_acc[k, 0] * (1.0 / root)).astype(BF16).astype(F32)
        kv_acc[k, 1] = kv_acc[k, 1].astype(BF16).astype(F32)

        def add(j, k=k):
            g_copy(k, j, s).wait_recv()
            kv_acc[k] += g_recv[j, k].astype(F32)
        loop(s + 1, n_seq, add)
        dkv_ref[k] = kv_acc[k].astype(BF16)

    for off in range(1, n_dp):
        j = lax.rem(d + off, n_dp)
        slot_copy(o_all.at[j], o_all, o_ss, o_rs, "dp", j, d).wait_recv()
    for j in range(n_dp):
        wg_ref[j * part:(j + 1) * part] = o_all[j].astype(F32)

    for k in range(kvh):
        loop(s + 1, n_seq, lambda j: kv_copy(k, s, j).wait_send())
        loop(0, s, lambda j: g_copy(k, s, j).wait_send())
    for off in range(1, n_head):
        slot_copy(lg_all.at[h], lg_all, lg_ss, lg_rs, "head", h, lax.rem(h + off, n_head)).wait_send()
    for off in range(1, n_dp):
        j = lax.rem(d + off, n_dp)
        slot_copy(w_send.at[j], w_recv, w_ss, w_rs, "dp", d, j).wait_send()
        slot_copy(o_all.at[d], o_all, o_ss, o_rs, "dp", d, j).wait_send()
    for off in range(1, n_seq):
        slot_copy(x_all.at[s], x_all, x_ss, x_rs, "seq", s, lax.rem(s + off, n_seq)).wait_send()


def on_device(
    queries, keys, values, attn_out, out_grad, gate_values, log_totals, hidden,
    block_ids, block_valid,
):
    toks, heads, dh = queries.shape[1:]
    kvh = keys.shape[2]
    tiles, nsel = block_ids.shape[1], block_ids.shape[3]
    group = heads // kvh
    blk = toks // tiles
    rows = blk * group
    n_seq, n_head, n_dp = (lax.axis_size(a) for a in ("seq", "head", "dp"))
    hq = n_head * heads
    width = hidden.shape[2]
    part = hq // n_dp
    dims = (n_seq, n_head, n_dp, tiles, blk, kvh, group, dh, nsel)
    kv = jnp.transpose(jnp.stack([keys[0], values[0]]), (2, 0, 1, 3))
    vm = pl.BlockSpec(memory_space=pltpu.VMEM)
    sm = pl.BlockSpec(memory_space=pltpu.SMEM)
    dma = pltpu.SemaphoreType.DMA
    qg, dkv, wg = pl.pallas_call(
        functools.partial(kernel, dims),
        out_shape=(
            jax.ShapeDtypeStruct((toks, heads, dh), BF16),
            jax.ShapeDtypeStruct((kvh, 2, toks, dh), BF16),
            jax.ShapeDtypeStruct((hq, width), F32),
        ),
        in_specs=[sm, sm] + [vm] * 7,
        out_specs=(vm, vm, vm),
        scratch_shapes=[
            pltpu.VMEM((toks, 128), F32),
            pltpu.VMEM((toks, 128), F32),
            pltpu.VMEM((tiles, kvh, rows, 2 * dh), BF16),
            pltpu.VMEM((tiles, kvh, rows, 2 * dh), BF16),
            pltpu.VMEM((tiles, kvh, rows, dh), F32),
            pltpu.VMEM((n_seq, kvh, 2, toks, dh), BF16),
            pltpu.VMEM((kvh, 2, toks, dh), F32),
            pltpu.VMEM((n_seq, kvh, 2, toks, dh), BF16),
            pltpu.VMEM((n_seq, kvh, 2, toks, dh), BF16),
            pltpu.VMEM((n_head, heads, toks), BF16),
            pltpu.VMEM((n_dp, part, width), F32),
            pltpu.VMEM((n_dp, part, width), BF16),
            pltpu.VMEM((n_dp, part, width), BF16),
            pltpu.VMEM((n_seq, part, width), BF16),
            pltpu.VMEM((n_dp, part, width), BF16),
            dma((n_seq, kvh)), dma((n_seq, kvh)), dma((n_seq, kvh)), dma((n_seq, kvh)),
            dma((n_head,)), dma((n_head,)), dma((n_dp,)), dma((n_dp,)),
            dma((n_seq,)), dma((n_seq,)), dma((n_dp,)), dma((n_dp,)),
        ],
        compiler_params=pltpu.CompilerParams(
            collective_id=0, has_side_effects=True, vmem_limit_bytes=60 * 1024 * 1024),
        name="attention_backward",
    )(block_ids[0], block_valid[0], queries[0], attn_out[0], out_grad[0],
      gate_values[0], log_totals[0], hidden[0], kv)
    key_grad = jnp.transpose(dkv[:, 0], (1, 0, 2))[None]
    value_grad = jnp.transpose(dkv[:, 1], (1, 0, 2))[None]
    return qg[None], key_grad, value_grad, wg


def solution(mesh):
    return jax.shard_map(
        on_device,
        mesh=mesh,
        in_specs=(
            P("dp", "seq", "head", None),
            P("dp", "seq", "head", None),
            P("dp", "seq", "head", None),
            P("dp", "seq", "head", None),
            P("dp", "seq", "head", None),
            P("dp", "head", "seq"),
            P("dp", "head", "seq"),
            P("dp", "seq", "head"),
            P("dp", "seq", "head", None),
            P("dp", "seq", "head", None),
        ),
        out_specs=(
            P("dp", "seq", "head", None),
            P("dp", "seq", "head", None),
            P("dp", "seq", "head", None),
            P(None, "head"),
        ),
        check_vma=False,
    )
```

time: 181 us -> 34.9 us (0.19)
  matrix products: 40.9 us -> 0 us
  waiting for transfers between devices: 35.1 us -> 0 us
  other arithmetic: 35.2 us -> 0.73 us
  Pallas kernels: 0 us -> 27.8 us
  blocking collectives: 26.4 us -> 0 us
  local copies, waits for them, and re-layouts: 24.1 us -> 5.53 us
  between operations: 15.6 us -> 0.68 us
  loops' own time: 2.88 us -> 0 us
    dot_general x21 -> x0, matrix products: 40.9 us -> none  [the longest x4 16.1 us: tile_math(): jnp.einsum('ikgd,knjd->kginj', grad_output, value_tile, preferred_element...]
    psum x1 -> x0, waiting for transfers between devices: 35.1 us -> none  [on_device(): gate_weight_grad = lax.psum(weight_part, ('seq', 'dp')) * weight_scale]
    pallas_call x0 -> x1, Pallas kernels: none -> 27.8 us  [on_device(): pl.pallas_call(functools.partial(kernel, dims), out_shape=(jax.ShapeDtype...]
    all_gather x3 -> x0, blocking collectives: 26.4 us -> none  [the longest x1 13.6 us: on_device(): every_logit = lax.all_gather(logit_rows, 'head', axis=1, tiled=True)]
    scatter-add x1 -> x0, other arithmetic: 19.1 us -> none  [on_device(): holder = holder.at[target, :, head_rows, :].add(paired_all, mode='drop')]
    dynamic_slice x16 -> x0, local copies, waits for them, and re-layouts: 10.6 us -> none  [on_device(): lax.scan(tile_step, jnp.zeros((), jnp.float32), tile_items)]
    dynamic_update_slice x8 -> x0, other arithmetic: 5.93 us -> none  [on_device(): lax.scan(tile_step, jnp.zeros((), jnp.float32), tile_items)]
    mul x5 -> x0, other arithmetic: 4.47 us -> none  [the longest x4 2.75 us: tile_math(): key_pos = picked[..., None] * block_rows + offsets]
  transfers between devices with their start and end apart: 2 -> 0, of which waited for: 1 -> 0; matrix products, arithmetic and copies ran while one was open for 12% -> 0% of each run, Pallas kernels for 0% -> 0%
where the time goes in v1:
time: 34.9 us; the launch traced here: 34.7 us
  Pallas kernels  27.8 us (80%)
  local copies, waits for them, and re-layouts  5.53 us (16%)
  other arithmetic  0.73 us (2%)
  between operations  0.68 us (2%)
    pallas_call x1, Pallas kernels, on_device(): pl.pallas_call(functools.partial(kernel, dims), out_shape=(jax.ShapeDtype...  27.8 us
    unnamed x12, local copies, waits for them, and re-layouts  4.45 us
    broadcast_in_dim x1, local copies, waits for them, and re-layouts, on_device(): value_grad = jnp.transpose(dkv[:, 1], (1, 0, 2))[None]  1.08 us
    transpose x1, other arithmetic, on_device(): kv = jnp.transpose(jnp.stack([keys[0], values[0]]), (2, 0, 1, 3))  0.73 us

profile of v1, /device:TPU:0, one launch (start us, length us, event | category | flops | bytes accessed | tf_op | source)
XLA Modules:
  0.0 34.7 jit_solution(1747748201869385545)
XLA Ops:
  0.6 0.0 copy-start.2
  0.6 1.0 %copy.14 = bf16[1,256,2,128]{3,1,0,2:T(8,128)(2,1)S(1)} copy(bf16[1,256,2,128]{3,2,1,0:T(2,128)(2,1)} %param.11) | data formatting | bytes 262144 | tf_op args[1]
  1.6 0.0 copy-done.2
  1.6 0.7 %maximum_bitcast_fusion.kv_ref = bf16[2,2,256,128]{3,2,1,0:T(8,128)(2,1)} fusion(bf16[1,256,2,128]{3,1,0,2:T(8,128)(2,1)S(1)} %copy.15, bf16[1,256,2,128]{3,1,0,2:T(8,128)(2,1)S(1)} %copy.14), kind=kLoop, calls=%fused_computation | loop fusion | flops 131072 | bytes 524288 | tf_op jit(solution)/shard_map/transpose | solution.py:279
  2.4 27.8 %attention_backward.1 = (bf16[256,16,128]{2,1,0:T(8,128)(2,1)}, bf16[2,2,256,128]{3,2,1,0:T(8,128)(2,1)}, f32[64,1280]{1,0:T(8,128)}) custom-call(s32[4,2,16]{2,1,0:T(2,128)} %bitcast.30, s32[4,2,16]{2,1,0:T(2,128)} %bitcast.31, bf16[256,16,128]{2,1,0:T(8,128)(2,1)} %bitcast.24, bf16[256,16,128]{2,1,0:T(8,128)(2,1)} %bitcast.25, ...), custom_call_target="tpu_custom_call" | custom-call | tf_op jit(solution)/shard_map/attention_backward/pallas_call | solution.py:283
  30.1 0.0 copy-start
  30.2 1.1 %slice_bitcast_fusion = (bf16[1,256,2,128]{3,1,2,0:T(8,128)(2,1)S(1)}, bf16[1,256,2,128]{3,1,2,0:T(8,128)(2,1)S(1)}) fusion(bf16[2,2,256,128]{3,2,1,0:T(8,128)(2,1)} %get-tuple-element.8), kind=kLoop, calls=%fused_computation.1 | loop fusion | bytes 524288 | tf_op jit(solution)/shard_map/broadcast_in_dim | solution.py:318
  31.2 0.8 %copy.17 = bf16[1,256,2,128]{3,2,1,0:T(2,128)(2,1)} copy(bf16[1,256,2,128]{3,1,2,0:T(8,128)(2,1)S(1)} %get-tuple-element.14) | data formatting | bytes 262144
  32.0 0.8 %copy.16 = bf16[1,256,2,128]{3,2,1,0:T(2,128)(2,1)} copy(bf16[1,256,2,128]{3,1,2,0:T(8,128)(2,1)S(1)} %get-tuple-element.15) | data formatting | bytes 262144
  32.8 0.0 copy-done
  32.8 0.0 copy-start.1
  32.8 1.0 %copy.20 = bf16[1,256,16,128]{3,2,1,0:T(8,128)(2,1)} copy(bf16[1,256,16,128]{3,2,1,0:T(8,128)(2,1)S(1)} %bitcast.23) | data formatting | bytes 2097152
  33.8 0.2 copy-done.1
  34.0 0.7 %copy.21 = f32[64,1280]{1,0:T(8,128)} copy(f32[64,1280]{1,0:T(8,128)S(1)} %copy-done.1) | data formatting | bytes 655360
  (1 shorter events, 0.0 us)
Async XLA Ops:
  0.6 1.0 %copy-start.2 = (bf16[1,256,2,128]{3,2,1,0:T(2,128)(2,1)S(1)}, bf16[1,256,2,128]{3,2,1,0:T(2,128)(2,1)}, u32[]{:S(2)}) copy-start(bf16[1,256,2,128]{3,2,1,0:T(2,128)(2,1)} %param.12) | copy-start | bytes 393220
  30.1 2.7 %copy-start = (bf16[256,16,128]{2,1,0:T(8,128)(2,1)S(1)}, bf16[256,16,128]{2,1,0:T(8,128)(2,1)}, u32[]{:S(2)}) copy-start(bf16[256,16,128]{2,1,0:T(8,128)(2,1)} %get-tuple-element.7) | copy-start | bytes 3145732
  32.8 1.2 %copy-start.1 = (f32[64,1280]{1,0:T(8,128)S(1)}, f32[64,1280]{1,0:T(8,128)}, u32[]{:S(2)}) copy-start(f32[64,1280]{1,0:T(8,128)} %get-tuple-element.23) | copy-start | bytes 983044

commit v2 on v1

--- a/solution.py
+++ b/solution.py
@@ -29,9 +29,9 @@
 
 def kernel(
     dims,
-    ids_ref, valid_ref, q_ref, ao_ref, og_ref, gate_ref, tot_ref, hid_ref, kv_ref,
-    qg_ref, dkv_ref, wg_ref,
-    cols, lgt, qaug, doaug, dq_acc, kv_in, kv_acc, g_send, g_recv,
+    ids_ref, valid_ref, q_hbm, ao_hbm, og_hbm, hid_hbm, gate_ref, tot_ref, k_ref, v_ref,
+    qg_hbm, dk_ref, dv_ref, wg_ref,
+    q_ref, ao_ref, og_ref, hid_ref, qg_ref, in_s, hid_s, qg_s, cols, lgt, qaug, doaug, dq_acc, kv_in, kv_acc, g_send, g_recv,
     lg_all, w_own, w_send, w_recv, x_all, o_all,
     kv_ss, kv_rs, g_ss, g_rs, lg_ss, lg_rs, w_ss, w_rs, x_ss, x_rs, o_ss, o_rs,
 ):
@@ -45,18 +45,33 @@
     root = math.sqrt(dh)
     cexp = math.log2(math.e) / root
 
+    def fetch(i, t):
+        src, dst = ((og_hbm, og_ref), (ao_hbm, ao_ref), (q_hbm, q_ref))[i]
+        at = pl.ds(t * blk, blk)
+        return pltpu.make_async_copy(src.at[at], dst.at[at], in_s.at[i, t])
+
+    hid_copy = pltpu.make_async_copy(hid_hbm, hid_ref, hid_s)
+
+    def put(t):
+        at = pl.ds(t * blk, blk)
+        return pltpu.make_async_copy(qg_ref.at[at], qg_hbm.at[at], qg_s.at[t])
+
     barrier = pltpu.get_barrier_semaphore()
     for name, me, n in (("seq", s, n_seq), ("head", h, n_head), ("dp", d, n_dp)):
         for off in range(1, n):
             pl.semaphore_signal(
                 barrier, inc=1, device_id={name: lax.rem(me + off, n)},
                 device_id_type=pl.DeviceIdType.MESH)
+    for t in range(tiles):
+        for i in range(3):
+            fetch(i, t).start()
+    hid_copy.start()
     pl.semaphore_wait(barrier, n_seq + n_head + n_dp - 3)
 
-    def kv_copy(k, src_s, dst_s):
+    def kv_copy(k, c, src_s, dst_s):
         return pltpu.make_async_remote_copy(
-            src_ref=kv_ref.at[k], dst_ref=kv_in.at[src_s, k],
-            send_sem=kv_ss.at[dst_s, k], recv_sem=kv_rs.at[src_s, k],
+            src_ref=(k_ref, v_ref)[c].at[k], dst_ref=kv_in.at[src_s, k, c],
+            send_sem=kv_ss.at[dst_s, k, c], recv_sem=kv_rs.at[src_s, k, c],
             device_id={"seq": dst_s}, device_id_type=pl.DeviceIdType.MESH)
 
     def g_copy(k, src_s, dst_s):
@@ -78,54 +93,58 @@
         lax.fori_loop(lo, hi, step, 0)
 
     for k in range(kvh):
-        loop(s + 1, n_seq, lambda j: kv_copy(k, s, j).start())
+        for c in range(2):
+            loop(s + 1, n_seq, lambda j: kv_copy(k, c, s, j).start())
 
     hi, mid, lo = split3(tot_ref[...] * (-root))
     stack = jnp.concatenate(
         [gate_ref[...], hi, mid, lo, jnp.zeros((128 - 4 * heads, toks), F32)], axis=0)
     cols[...] = jnp.transpose(stack)
 
-    lane = lax.broadcasted_iota(jnp.int32, (rows, 128), 1)
-    g_of = lax.rem(lax.broadcasted_iota(jnp.int32, (rows, 128), 0), group)
+    lane = lax.broadcasted_iota(jnp.int32, (1, group, 128), 2)
+    g_of = lax.broadcasted_iota(jnp.int32, (1, group, 128), 1)
     pick = (
         lax.broadcasted_iota(jnp.int32, (blk, rows), 0)
         == lax.broadcasted_iota(jnp.int32, (blk, rows), 1) // group
     ).astype(BF16)
-    lane1 = lax.broadcasted_iota(jnp.int32, (1, 128), 1)
 
     def prep(t):
         at = pl.ds(pl.multiple_of(t * blk, blk), blk)
+        for i in range(3):
+            fetch(i, t).wait()
         og = og_ref[at].astype(F32)
         ao = ao_ref[at].astype(F32)
         q = q_ref[at].astype(F32)
-        wide = jnp.broadcast_to(cols[at][:, None, :], (blk, group, 128)).reshape(rows, 128)
-        x = jnp.zeros((rows, 128), F32)
+        wide = jnp.broadcast_to(cols[at][:, None, :], (blk, group, 128))
+        x = jnp.zeros((blk, group, 128), F32)
         for k in range(kvh):
             part = slice(k * group, (k + 1) * group)
-            ogk = og[:, part, :].reshape(rows, dh)
-            aok = ao[:, part, :].reshape(rows, dh)
-            qk = q[:, part, :].reshape(rows, dh)
-            mine = lax.rem(lane, heads) == g_of + k * group
-            sel = jnp.full((1, 128), MASKED, F32)
+            ogk, aok, qk = og[:, part, :], ao[:, part, :], q[:, part, :]
+            head = g_of + k * group
+            mine = lax.rem(lane, heads) == head
+            sel = jnp.full((1, group, 128), MASKED, F32)
             for n in range(nsel):
                 b = jnp.where(valid_ref[t, k, n] > 0, ids_ref[t, k, n], -1000)
-                sel = jnp.where(lane1 == b + 4 * heads, 0.0, sel)
-            gate = jnp.sum(jnp.where(mine & (lane < heads), wide, 0.0), axis=1, keepdims=True)
+                sel = jnp.where(lane == b + 4 * heads, 0.0, sel)
+            gate = jnp.sum(jnp.where(lane == head, wide, 0.0), axis=2, keepdims=True)
             tail = jnp.where(
                 lane >= 4 * heads, sel, jnp.where(mine & (lane >= heads), wide, 0.0))
-            qaug[t, k, :, :dh] = qk.astype(BF16)
-            qaug[t, k, :, dh:] = tail.astype(BF16)
-            go = (gate * ogk).astype(BF16)
-            dl_hi, dl_mid, dl_lo = split3(
-                -jnp.sum(go.astype(F32) * aok, axis=1, keepdims=True))
+            qaug[t, k, :, :dh] = qk.reshape(rows, dh).astype(BF16)
+            qaug[t, k, :, dh:] = tail.reshape(rows, 128).astype(BF16)
+            go = (gate * ogk).reshape(rows, dh).astype(BF16)
+            wide_go = go.astype(F32).reshape(blk, group, dh)
+            dl_hi, dl_mid, dl_lo = split3(-jnp.sum(wide_go * aok, axis=2, keepdims=True))
             doaug[t, k, :, :dh] = go
             doaug[t, k, :, dh:] = jnp.where(
                 lane == heads, dl_hi,
                 jnp.where(lane == heads + 1, dl_mid,
-                          jnp.where(lane == heads + 2, dl_lo, 0.0))).astype(BF16)
-            lg = jnp.sum(ogk * aok, axis=1, keepdims=True) * gate * (1.0 - gate)
-            x = x + jnp.where(lane == g_of + k * group, lg, 0.0)
-        lgt[at, :] = mm(pick, x.astype(BF16), NN)
+                          jnp.where(lane == heads + 2, dl_lo, 0.0))
+            ).reshape(rows, 128).astype(BF16)
+            lg = jnp.sum(ogk * aok, axis=2, keepdims=True) * gate * (1.0 - gate)
+            x = x + jnp.where(lane == head, lg, 0.0)
+            if k > 0:
+                dq_acc[t, k] = jnp.zeros((rows, dh), F32)
+        lgt[at, :] = mm(pick, x.reshape(rows, 128).astype(BF16), NN)
 
     loop(0, tiles, prep)
     lg_all[h] = jnp.transpose(lgt[...])[:heads].astype(BF16)
@@ -160,8 +179,11 @@
     def local(k):
         for t in range(tiles - 1, -1, -1):
             nk = (t + 1) * blk
-            dq, dk, dv = pair(kv_ref[k, 0, :nk], kv_ref[k, 1, :nk], own_tail[:nk], t, k, True)
-            dq_acc[t, k] = dq
+            dq, dk, dv = pair(k_ref[k, :nk], v_ref[k, :nk], own_tail[:nk], t, k, True)
+            if k == 0:
+                dq_acc[t, k] = dq
+            else:
+                dq_acc[t, k] += dq
             if t == tiles - 1:
                 kv_acc[k, 0] = dk
                 kv_acc[k, 1] = dv
@@ -172,7 +194,8 @@
     def remote(k):
         def one(i):
             r = s - 1 - i
-            kv_copy(k, r, s).wait_recv()
+            for c in range(2):
+                kv_copy(k, c, r, s).wait_recv()
             tail = key_tail(r)
             kk = kv_in[r, k, 0]
             vv = kv_in[r, k, 1]
@@ -187,12 +210,12 @@
             g_copy(k, s, r).start()
         loop(0, s, one)
 
-    for k in range(kvh):
-        local(k)
+    local(0)
 
     for off in range(1, n_head):
         j = lax.rem(h + off, n_head)
         slot_copy(lg_all.at[j], lg_all, lg_ss, lg_rs, "head", j, h).wait_recv()
+    hid_copy.wait()
     hq = n_head * heads
     w = mm(lg_all[...].reshape(hq, toks), hid_ref[...], NN)
     part = hq // n_dp
@@ -227,10 +250,13 @@
     for off in range(1, n_dp):
         slot_copy(o_all.at[d], o_all, o_ss, o_rs, "dp", d, lax.rem(d + off, n_dp)).start()
 
+    for k in range(1, kvh):
+        local(k)
     for t in range(tiles):
         qg_ref[t * blk:(t + 1) * blk] = jnp.concatenate(
             [dq_acc[t, k].reshape(blk, group, dh) for k in range(kvh)], axis=1
         ).__mul__(1.0 / root).astype(BF16)
+        put(t).start()
 
     for k in range(kvh):
         kv_acc[k, 0] = (kv_acc[k, 0] * (1.0 / root)).astype(BF16).astype(F32)
@@ -240,16 +266,20 @@
             g_copy(k, j, s).wait_recv()
             kv_acc[k] += g_recv[j, k].astype(F32)
         loop(s + 1, n_seq, add)
-        dkv_ref[k] = kv_acc[k].astype(BF16)
+        dk_ref[k] = kv_acc[k, 0].astype(BF16)
+        dv_ref[k] = kv_acc[k, 1].astype(BF16)
 
     for off in range(1, n_dp):
         j = lax.rem(d + off, n_dp)
         slot_copy(o_all.at[j], o_all, o_ss, o_rs, "dp", j, d).wait_recv()
     for j in range(n_dp):
-        wg_ref[j * part:(j + 1) * part] = o_all[j].astype(F32)
+        wg_ref[j] = o_all[j]
+    for t in range(tiles):
+        put(t).wait()
 
     for k in range(kvh):
-        loop(s + 1, n_seq, lambda j: kv_copy(k, s, j).wait_send())
+        for c in range(2):
+            loop(s + 1, n_seq, lambda j: kv_copy(k, c, s, j).wait_send())
         loop(0, s, lambda j: g_copy(k, s, j).wait_send())
     for off in range(1, n_head):
         slot_copy(lg_all.at[h], lg_all, lg_ss, lg_rs, "head", h, lax.rem(h + off, n_head)).wait_send()
@@ -276,20 +306,27 @@
     width = hidden.shape[2]
     part = hq // n_dp
     dims = (n_seq, n_head, n_dp, tiles, blk, kvh, group, dh, nsel)
-    kv = jnp.transpose(jnp.stack([keys[0], values[0]]), (2, 0, 1, 3))
+    any_ = pl.BlockSpec(memory_space=pl.ANY)
     vm = pl.BlockSpec(memory_space=pltpu.VMEM)
     sm = pl.BlockSpec(memory_space=pltpu.SMEM)
     dma = pltpu.SemaphoreType.DMA
-    qg, dkv, wg = pl.pallas_call(
+    qg, dk, dv, wg = pl.pallas_call(
         functools.partial(kernel, dims),
         out_shape=(
             jax.ShapeDtypeStruct((toks, heads, dh), BF16),
-            jax.ShapeDtypeStruct((kvh, 2, toks, dh), BF16),
-            jax.ShapeDtypeStruct((hq, width), F32),
+            jax.ShapeDtypeStruct((kvh, toks, dh), BF16),
+            jax.ShapeDtypeStruct((kvh, toks, dh), BF16),
+            jax.ShapeDtypeStruct((n_dp, part, width), BF16),
         ),
-        in_specs=[sm, sm] + [vm] * 7,
-        out_specs=(vm, vm, vm),
+        in_specs=[sm, sm] + [any_] * 4 + [vm] * 4,
+        out_specs=(any_, vm, vm, vm),
         scratch_shapes=[
+            pltpu.VMEM((toks, heads, dh), BF16),
+            pltpu.VMEM((toks, heads, dh), BF16),
+            pltpu.VMEM((toks, heads, dh), BF16),
+            pltpu.VMEM((toks, width), BF16),
+            pltpu.VMEM((toks, heads, dh), BF16),
+            dma((3, tiles)), dma, dma((tiles,)),
             pltpu.VMEM((toks, 128), F32),
             pltpu.VMEM((toks, 128), F32),
             pltpu.VMEM((tiles, kvh, rows, 2 * dh), BF16),
@@ -305,18 +342,19 @@
             pltpu.VMEM((n_dp, part, width), BF16),
             pltpu.VMEM((n_seq, part, width), BF16),
             pltpu.VMEM((n_dp, part, width), BF16),
-            dma((n_seq, kvh)), dma((n_seq, kvh)), dma((n_seq, kvh)), dma((n_seq, kvh)),
+            dma((n_seq, kvh, 2)), dma((n_seq, kvh, 2)), dma((n_seq, kvh)), dma((n_seq, kvh)),
             dma((n_head,)), dma((n_head,)), dma((n_dp,)), dma((n_dp,)),
             dma((n_seq,)), dma((n_seq,)), dma((n_dp,)), dma((n_dp,)),
         ],
         compiler_params=pltpu.CompilerParams(
-            collective_id=0, has_side_effects=True, vmem_limit_bytes=60 * 1024 * 1024),
+            collective_id=0, has_side_effects=True, vmem_limit_bytes=67043328),
         name="attention_backward",
-    )(block_ids[0], block_valid[0], queries[0], attn_out[0], out_grad[0],
-      gate_values[0], log_totals[0], hidden[0], kv)
-    key_grad = jnp.transpose(dkv[:, 0], (1, 0, 2))[None]
-    value_grad = jnp.transpose(dkv[:, 1], (1, 0, 2))[None]
-    return qg[None], key_grad, value_grad, wg
+    )(block_ids[0], block_valid[0], queries[0], attn_out[0], out_grad[0], hidden[0],
+      gate_values[0], log_totals[0],
+      jnp.transpose(keys[0], (1, 0, 2)), jnp.transpose(values[0], (1, 0, 2)))
+    key_grad = jnp.transpose(dk, (1, 0, 2))[None]
+    value_grad = jnp.transpose(dv, (1, 0, 2))[None]
+    return qg[None], key_grad, value_grad, wg.reshape(hq, width).astype(F32)
 
 
 def solution(mesh):

time: 34.9 us -> 33 us (0.946)
  Pallas kernels: 27.8 us -> 24.6 us
  local copies, waits for them, and re-layouts: 5.53 us -> 6.72 us
    pallas_call x1, Pallas kernels: 27.8 us -> 24.6 us  [on_device(): pl.pallas_call(functools.partial(kernel, dims), out_shape=(jax.ShapeDtype...]
    transpose x0 -> x1, local copies, waits for them, and re-layouts: none -> 1.7 us  [on_device(): jnp.transpose(values[0], (1, 0, 2))]
    broadcast_in_dim x1 -> x0, local copies, waits for them, and re-layouts: 1.08 us -> none  [on_device(): value_grad = jnp.transpose(dkv[:, 1], (1, 0, 2))[None]]
    convert_element_type x0 -> x1, other arithmetic: none -> 0.76 us  [on_device(): return (qg[None], key_grad, value_grad, wg.reshape(hq, width).astype(F32))]
    transpose x1 -> x0, other arithmetic: 0.73 us -> none  [on_device(): kv = jnp.transpose(jnp.stack([keys[0], values[0]]), (2, 0, 1, 3))]
    unnamed x12 -> x7, local copies, waits for them, and re-layouts: 4.45 us -> 5.02 us
where the time goes in v2:
time: 33 us; the launch traced here: 32.8 us
  Pallas kernels  24.6 us (75%)
  local copies, waits for them, and re-layouts  6.72 us (20%)
  other arithmetic  0.76 us (2%)
  between operations  0.65 us (2%)
    pallas_call x1, Pallas kernels, on_device(): pl.pallas_call(functools.partial(kernel, dims), out_shape=(jax.ShapeDtype...  24.6 us
    unnamed x7, local copies, waits for them, and re-layouts  5.02 us
    transpose x1, local copies, waits for them, and re-layouts, on_device(): jnp.transpose(values[0], (1, 0, 2))  1.7 us
    convert_element_type x1, other arithmetic, on_device(): return (qg[None], key_grad, value_grad, wg.reshape(hq, width).astype(F32))  0.76 us

profile of v2, /device:TPU:0, one launch (start us, length us, event | category | flops | bytes accessed | tf_op | source)
XLA Modules:
  0.0 32.8 jit_solution(16783803974516431244)
XLA Ops:
  0.6 1.7 %copy_bitcast_fusion = (bf16[2,256,128]{2,1,0:T(8,128)(2,1)}, bf16[2,256,128]{2,1,0:T(8,128)(2,1)}) fusion(bf16[1,256,2,128]{3,2,1,0:T(2,128)(2,1)} %param.12, bf16[1,256,2,128]{3,2,1,0:T(2,128)(2,1)} %param.11), kind=kLoop, calls=%fused_computation.1 | loop fusion | bytes 524288 | tf_op jit(solution)/shard_map/transpose | solution.py:354
  2.3 24.6 %attention_backward.1 = (bf16[256,16,128]{2,1,0:T(8,128)(2,1)}, bf16[2,256,128]{2,1,0:T(8,128)(2,1)}, bf16[2,256,128]{2,1,0:T(8,128)(2,1)}, bf16[4,16,1280]{2,1,0:T(8,128)(2,1)}) custom-call(s32[4,2,16]{2,1,0:T(2,128)} %bitcast.35, s32[4,2,16]{2,1,0:T(2,128)} %bitcast.36, bf16[256,16,128]{2,1,0:T(8,128)(2,1)} %bitcast.27, bf16[256,16,128]{2,1,0:T(8,128)(2,1)} %bitcast.28, ...), custom_call_target="tpu_custom_call" | custom-call | tf_op jit(solution)/shard_map/attention_backward/pallas_call | solution.py:313
  27.0 0.0 copy-start.1
  27.0 1.7 %copy.16 = bf16[1,256,2,128]{3,2,1,0:T(2,128)(2,1)} copy(bf16[1,256,2,128]{3,1,2,0:T(8,128)(2,1)} %bitcast.32) | data formatting | bytes 262144
  28.7 0.0 copy-done.1
  28.7 0.0 copy-start
  28.7 0.8 %copy.17 = bf16[1,256,2,128]{3,2,1,0:T(2,128)(2,1)} copy(bf16[1,256,2,128]{3,1,2,0:T(8,128)(2,1)S(1)} %bitcast.31) | data formatting | bytes 262144
  29.5 0.1 copy-done
  29.6 0.8 %bitcast_convert_fusion = f32[64,1280]{1,0:T(8,128)} fusion(bf16[4,16,1280]{2,1,0:T(8,128)(2,1)S(1)} %copy-done), kind=kLoop, calls=%fused_computation | loop fusion | flops 81920 | bytes 491520 | tf_op jit(solution)/shard_map/convert_element_type | solution.py:357
  30.4 2.4 %copy.21 = bf16[1,256,16,128]{3,2,1,0:T(8,128)(2,1)} copy(bf16[1,256,16,128]{3,2,1,0:T(8,128)(2,1)} %bitcast.26) | data formatting | bytes 2097152
Async XLA Ops:
  27.0 1.7 %copy-start.1 = (bf16[2,256,128]{2,1,0:T(8,128)(2,1)S(1)}, bf16[2,256,128]{2,1,0:T(8,128)(2,1)}, u32[]{:S(2)}) copy-start(bf16[2,256,128]{2,1,0:T(8,128)(2,1)} %get-tuple-element.10) | copy-start | bytes 393220
  28.7 0.9 %copy-start = (bf16[4,16,1280]{2,1,0:T(8,128)(2,1)S(1)}, bf16[4,16,1280]{2,1,0:T(8,128)(2,1)}, u32[]{:S(2)}) copy-start(bf16[4,16,1280]{2,1,0:T(8,128)(2,1)} %get-tuple-element.11) | copy-start | bytes 491524

commit v3 on v2

--- a/solution.py
+++ b/solution.py
@@ -29,9 +29,9 @@
 
 def kernel(
     dims,
-    ids_ref, valid_ref, q_hbm, ao_hbm, og_hbm, hid_hbm, gate_ref, tot_ref, k_ref, v_ref,
-    qg_hbm, dk_ref, dv_ref, wg_ref,
-    q_ref, ao_ref, og_ref, hid_ref, qg_ref, in_s, hid_s, qg_s, cols, lgt, qaug, doaug, dq_acc, kv_in, kv_acc, g_send, g_recv,
+    ids_ref, valid_ref, q_hbm, ao_hbm, og_hbm, hid_hbm, gate_ref, tot_ref, k_raw, v_raw,
+    qg_ref, dk_ref, dv_ref, wg_ref,
+    q_ref, ao_ref, og_ref, hid_ref, k_ref, v_ref, in_s, hid_s, cols, lgt, qaug, doaug, dq_acc, kv_in, kv_acc, g_send, g_recv,
     lg_all, w_own, w_send, w_recv, x_all, o_all,
     kv_ss, kv_rs, g_ss, g_rs, lg_ss, lg_rs, w_ss, w_rs, x_ss, x_rs, o_ss, o_rs,
 ):
@@ -52,10 +52,6 @@
 
     hid_copy = pltpu.make_async_copy(hid_hbm, hid_ref, hid_s)
 
-    def put(t):
-        at = pl.ds(t * blk, blk)
-        return pltpu.make_async_copy(qg_ref.at[at], qg_hbm.at[at], qg_s.at[t])
-
     barrier = pltpu.get_barrier_semaphore()
     for name, me, n in (("seq", s, n_seq), ("head", h, n_head), ("dp", d, n_dp)):
         for off in range(1, n):
@@ -66,6 +62,10 @@
         for i in range(3):
             fetch(i, t).start()
     hid_copy.start()
+    for raw, ref in ((k_raw, k_ref), (v_raw, v_ref)):
+        wide = raw[...].astype(F32)
+        for k in range(kvh):
+            ref[k] = wide[:, k, :].astype(BF16)
     pl.semaphore_wait(barrier, n_seq + n_head + n_dp - 3)
 
     def kv_copy(k, c, src_s, dst_s):
@@ -256,7 +256,6 @@
         qg_ref[t * blk:(t + 1) * blk] = jnp.concatenate(
             [dq_acc[t, k].reshape(blk, group, dh) for k in range(kvh)], axis=1
         ).__mul__(1.0 / root).astype(BF16)
-        put(t).start()
 
     for k in range(kvh):
         kv_acc[k, 0] = (kv_acc[k, 0] * (1.0 / root)).astype(BF16).astype(F32)
@@ -274,8 +273,6 @@
         slot_copy(o_all.at[j], o_all, o_ss, o_rs, "dp", j, d).wait_recv()
     for j in range(n_dp):
         wg_ref[j] = o_all[j]
-    for t in range(tiles):
-        put(t).wait()
 
     for k in range(kvh):
         for c in range(2):
@@ -289,6 +286,22 @@
         slot_copy(o_all.at[d], o_all, o_ss, o_rs, "dp", d, j).wait_send()
     for off in range(1, n_seq):
         slot_copy(x_all.at[s], x_all, x_ss, x_rs, "seq", s, lax.rem(s + off, n_seq)).wait_send()
+
+
+def finish(qg_ref, dk_ref, dv_ref, wg_ref, qo, ko, vo, wo, kbuf, vbuf, wbuf, sems):
+    copies = [pltpu.make_async_copy(a, b, sems.at[i]) for i, (a, b) in enumerate(
+        ((qg_ref, qo), (kbuf, ko), (vbuf, vo), (wbuf, wo)))]
+    copies[0].start()
+    part = wg_ref.shape[1]
+    for j in range(wg_ref.shape[0]):
+        wbuf[j * part:(j + 1) * part] = wg_ref[j].astype(F32)
+    copies[3].start()
+    for i, src, dst in ((1, dk_ref, kbuf), (2, dv_ref, vbuf)):
+        dst[...] = jnp.concatenate(
+            [src[k].astype(F32)[:, None, :] for k in range(src.shape[0])], axis=1).astype(BF16)
+        copies[i].start()
+    for c in copies:
+        c.wait()
 
 
 def on_device(
@@ -313,20 +326,21 @@
     qg, dk, dv, wg = pl.pallas_call(
         functools.partial(kernel, dims),
         out_shape=(
-            jax.ShapeDtypeStruct((toks, heads, dh), BF16),
-            jax.ShapeDtypeStruct((kvh, toks, dh), BF16),
-            jax.ShapeDtypeStruct((kvh, toks, dh), BF16),
-            jax.ShapeDtypeStruct((n_dp, part, width), BF16),
+            pltpu.VMEM((toks, heads, dh), BF16),
+            pltpu.VMEM((kvh, toks, dh), BF16),
+            pltpu.VMEM((kvh, toks, dh), BF16),
+            pltpu.VMEM((n_dp, part, width), BF16),
         ),
         in_specs=[sm, sm] + [any_] * 4 + [vm] * 4,
-        out_specs=(any_, vm, vm, vm),
+        out_specs=(vm, vm, vm, vm),
         scratch_shapes=[
             pltpu.VMEM((toks, heads, dh), BF16),
             pltpu.VMEM((toks, heads, dh), BF16),
             pltpu.VMEM((toks, heads, dh), BF16),
             pltpu.VMEM((toks, width), BF16),
-            pltpu.VMEM((toks, heads, dh), BF16),
-            dma((3, tiles)), dma, dma((tiles,)),
+            pltpu.VMEM((kvh, toks, dh), BF16),
+            pltpu.VMEM((kvh, toks, dh), BF16),
+            dma((3, tiles)), dma,
             pltpu.VMEM((toks, 128), F32),
             pltpu.VMEM((toks, 128), F32),
             pltpu.VMEM((tiles, kvh, rows, 2 * dh), BF16),
@@ -347,14 +361,31 @@
             dma((n_seq,)), dma((n_seq,)), dma((n_dp,)), dma((n_dp,)),
         ],
         compiler_params=pltpu.CompilerParams(
-            collective_id=0, has_side_effects=True, vmem_limit_bytes=67043328),
+            collective_id=0, has_side_effects=True, vmem_limit_bytes=62 * 1024 * 1024),
         name="attention_backward",
     )(block_ids[0], block_valid[0], queries[0], attn_out[0], out_grad[0], hidden[0],
       gate_values[0], log_totals[0],
-      jnp.transpose(keys[0], (1, 0, 2)), jnp.transpose(values[0], (1, 0, 2)))
-    key_grad = jnp.transpose(dk, (1, 0, 2))[None]
-    value_grad = jnp.transpose(dv, (1, 0, 2))[None]
-    return qg[None], key_grad, value_grad, wg.reshape(hq, width).astype(F32)
+      keys[0], values[0])
+    query_grad, key_grad, value_grad, weight_grad = pl.pallas_call(
+        finish,
+        out_shape=(
+            jax.ShapeDtypeStruct((toks, heads, dh), BF16),
+            jax.ShapeDtypeStruct((toks, kvh, dh), BF16),
+            jax.ShapeDtypeStruct((toks, kvh, dh), BF16),
+            jax.ShapeDtypeStruct((hq, width), F32),
+        ),
+        in_specs=[vm] * 4,
+        out_specs=(any_,) * 4,
+        scratch_shapes=[
+            pltpu.VMEM((toks, kvh, dh), BF16),
+            pltpu.VMEM((toks, kvh, dh), BF16),
+            pltpu.VMEM((hq, width), F32),
+            dma((4,)),
+        ],
+        compiler_params=pltpu.CompilerParams(vmem_limit_bytes=16 * 1024 * 1024),
+        name="write_outputs",
+    )(*(pltpu.with_memory_space_constraint(a, pltpu.VMEM) for a in (qg, dk, dv, wg)))
+    return query_grad[None], key_grad[None], value_grad[None], weight_grad
 
 
 def solution(mesh):

time: 33 us -> 25.9 us (0.78)
  local copies, waits for them, and re-layouts: 6.72 us -> 0 us
  other arithmetic: 0.76 us -> 0 us
  Pallas kernels: 24.6 us -> 25.1 us
    unnamed x7 -> x0, local copies, waits for them, and re-layouts: 5.02 us -> none
    transpose x1 -> x0, local copies, waits for them, and re-layouts: 1.7 us -> none  [on_device(): jnp.transpose(values[0], (1, 0, 2))]
    convert_element_type x1 -> x0, other arithmetic: 0.76 us -> none  [on_device(): return (qg[None], key_grad, value_grad, wg.reshape(hq, width).astype(F32))]
    pallas_call x1 -> x2, Pallas kernels: 24.6 us -> 25.1 us  [the longest x1 23.9 us: on_device(): pl.pallas_call(functools.partial(kernel, dims), out_shape=(pltpu.VMEM((to...]
where the time goes in v3:
time: 25.9 us; the launch traced here: 25.7 us
  Pallas kernels  25.1 us (97%)
  between operations  0.64 us (2%)
    pallas_call x1, Pallas kernels, on_device(): pl.pallas_call(functools.partial(kernel, dims), out_shape=(pltpu.VMEM((to...  23.9 us
    pallas_call x1, Pallas kernels, on_device(): pl.pallas_call(finish, out_shape=(jax.ShapeDtypeStruct((toks, heads, dh),...  1.19 us

profile of v3, /device:TPU:0, one launch (start us, length us, event | category | flops | bytes accessed | tf_op | source)
XLA Modules:
  0.0 25.7 jit_solution(834100271080262845)
XLA Ops:
  0.6 23.9 %attention_backward.1 = (bf16[256,16,128]{2,1,0:T(8,128)(2,1)S(1)}, bf16[2,256,128]{2,1,0:T(8,128)(2,1)S(1)}, bf16[2,256,128]{2,1,0:T(8,128)(2,1)S(1)}, bf16[4,16,1280]{2,1,0:T(8,128)(2,1)S(1)}) custom-call(s32[4,2,16]{2,1,0:T(2,128)} %bitcast.21, s32[4,2,16]{2,1,0:T(2,128)} %bitcast.22, bf16[256,16,128]{2,1,0:T(8,128)(2,1)} %bitcast.13, ...), custom_call_target="tpu_custom_call" | custom-call | tf_op jit(solution)/shard_map/attention_backward/pallas_call | solution.py:326
  24.5 1.2 %write_outputs.1 = (bf16[256,16,128]{2,1,0:T(8,128)(2,1)}, bf16[256,2,128]{2,1,0:T(2,128)(2,1)}, bf16[256,2,128]{2,1,0:T(2,128)(2,1)}, f32[64,1280]{1,0:T(8,128)}) custom-call(bf16[256,16,128]{2,1,0:T(8,128)(2,1)S(1)} %get-tuple-element.12.qg_ref, bf16[2,256,128]{2,1,0:T(8,128)(2,1)S(1)} %get-tuple-element.13.dk_ref, ...), custom_call_target="tpu_custom_call" | custom-call | tf_op jit(solution)/shard_map/write_outputs/pallas_call | solution.py:369
